TPU v7x, 32 devices: a whole 2x2x4 slice. The times are simulated.
32 devices in a mesh: dp: 2 (over x), ep_b: 4 (over z), ep_a: 4 (over y, core).
Axes of the slice: x: 2, y: 2, z: 4, core: 2. Of those that a mesh axis runs over, the one named last changes fastest.
Arguments:
- tokens: bfloat16 [32, 1024, 1024], P(('dp', 'ep_b', 'ep_a')), parts along dimension 0
- expert_ids: int32 [32, 1024], P(('dp', 'ep_b', 'ep_a')), parts along dimension 0
- route_order: int32 [32, 1024], P(('dp', 'ep_b', 'ep_a')), parts along dimension 0
- w_route: bfloat16 [1024, 256], replicated
- expert_keys: bfloat16 [16, 256], replicated
- temperature: float32 [], replicated
- w_in: bfloat16 [16, 1024, 4096], P(('ep_b', 'ep_a'))
- b_in: bfloat16 [16, 4096], P(('ep_b', 'ep_a'))
- w_out: bfloat16 [16, 4096, 1024], P(('ep_b', 'ep_a'))
- b_out: bfloat16 [16, 1024], P(('ep_b', 'ep_a'))
Outputs:
- output: bfloat16 [32, 1024, 1024], P(('dp', 'ep_b', 'ep_a')), parts along dimension 0
There are 2 independent parts. A program takes and returns all parts, laid end to end along the dimension named above; an argument that names none is the same for every part.
All inputs are finite; a program needn't handle non-finite values.
Results may differ from a plain program's by a relative error of at most 0.00349485.
Values are sent between devices in bfloat16 or wider.
A program may use at most 1 GiB of HBM per device.

v0:
```python
import jax
import jax.numpy as jnp
from jax import lax
from jax.sharding import PartitionSpec as P

EXPERT_AXES = ("ep_b", "ep_a")


def route_local(tok_rows, id_row, order_row, w_route, expert_keys, value_a11, capacity):
    num_experts = expert_keys.shape[0]
    tok_dev = tok_rows.shape[0]
    keys_f32 = expert_keys.astype(jnp.float32)
    key_unit = keys_f32 / jnp.sqrt(jnp.sum(keys_f32 * keys_f32, axis=1, keepdims=True))
    projected = jnp.dot(tok_rows, w_route, preferred_element_type=jnp.float32)
    proj_unit = projected / jnp.sqrt(jnp.sum(projected * projected, axis=1, keepdims=True))
    router_prob = jax.nn.softmax(jnp.dot(proj_unit, key_unit.T) / value_a11, axis=1)
    expert_range = jnp.arange(num_experts, dtype=jnp.int32)[None, :]
    gate_prob = jnp.sum(jnp.where(id_row[:, None] == expert_range, router_prob, 0.0), axis=1)
    ranked_ids = jnp.take(id_row, order_row)
    ranked_hot = (ranked_ids[:, None] == expert_range).astype(jnp.int32)
    ranked_pos = jnp.sum(jnp.cumsum(ranked_hot, axis=0) * ranked_hot, axis=1) - 1
    ranked_slot = jnp.where(ranked_pos < capacity, ranked_ids * capacity + ranked_pos, num_experts * capacity)
    slot_source = jnp.full((num_experts * capacity,), tok_dev, jnp.int32).at[ranked_slot].set(order_row, mode="drop")
    dest_slot = jnp.zeros((tok_dev,), jnp.int32).at[order_row].set(ranked_slot)
    send_rows = jnp.take(tok_rows, slot_source, axis=0, mode="fill", fill_value=0)
    return send_rows, gate_prob, dest_slot


def expert_local(slot_rows, w_first, b_first, w_second, b_second):
    hidden = jnp.dot(slot_rows, w_first, preferred_element_type=jnp.float32) + b_first.astype(jnp.float32)
    hidden = jax.nn.gelu(hidden, approximate=False).astype(jnp.bfloat16)
    result = jnp.dot(hidden, w_second, preferred_element_type=jnp.float32) + b_second.astype(jnp.float32)
    return result.astype(jnp.bfloat16)


def combine_local(back_rows, dest_slot, gate_prob):
    picked = jnp.take(back_rows, dest_slot, axis=0, mode="fill", fill_value=0)
    return (gate_prob[:, None] * picked.astype(jnp.float32)).astype(jnp.bfloat16)


def solution(mesh):
    num_experts = mesh.shape["ep_b"] * mesh.shape["ep_a"]
    tok_spec = P(("dp",) + EXPERT_AXES)
    expert_spec = P(EXPERT_AXES)

    def device_step(tokens, expert_ids, route_order, w_route, expert_keys, value_a11, w_in, b_in, w_out, b_out):
        tok_dev, model_width = tokens.shape[1], tokens.shape[2]
        capacity = (5 * tok_dev + 4 * num_experts - 1) // (4 * num_experts)
        send_rows, gate_prob, dest_slot = route_local(tokens[0], expert_ids[0], route_order[0], w_route, expert_keys, value_a11, capacity)
        arrived = lax.all_to_all(send_rows.reshape(num_experts, capacity, model_width), EXPERT_AXES, 0, 0, tiled=True)
        expert_rows = expert_local(arrived.reshape(num_experts * capacity, model_width), w_in[0], b_in[0], w_out[0], b_out[0])
        returned = lax.all_to_all(expert_rows.reshape(num_experts, capacity, model_width), EXPERT_AXES, 0, 0, tiled=True)
        return combine_local(returned.reshape(num_experts * capacity, model_width), dest_slot, gate_prob)[None]

    return jax.shard_map(
        device_step,
        mesh=mesh,
        in_specs=(tok_spec, tok_spec, tok_spec, P(), P(), P(), expert_spec, expert_spec, expert_spec, expert_spec),
        out_specs=tok_spec,
        check_vma=False,
    )
```

profile of v0, /device:TPU:15, one launch (start us, length us, event | category | flops | bytes accessed | tf_op | source)
XLA Modules:
  0.0 239.0 jit_solution(4064184244348995790)
XLA Ops:
  0.0 0.0 copy-start
  0.0 0.8 compare_select_fusion.1
  0.8 0.0 copy-start.3
  0.9 0.6 copy-done.3
  1.4 5.7 %gather_fusion = s32[1024]{0:T(1024)S(1)} fusion(s32[1024]{0:T(1024)} %bitcast.64, s32[1024]{0:T(1024)S(1)} %broadcast_clamp_fusion), kind=kCustom, calls=%fused_computation | custom fusion | bytes 12288 | tf_op jit(solution)/shard_map/jit(_take)/gather | solution.py:19
  7.2 0.7 bitcast_select_fusion.1
  7.9 4.5 %reduce-window.6 = s32[16,8,128]{2,1,0:T(8,128)S(1)} reduce-window(s32[16,8,128]{2,1,0:T(8,128)S(1)} %fusion.53, s32[]{:T(128)} %constant.42.clone.1), window={size=1x1x128 pad=0_0x0_0x127_0}, to_apply=%region_5.6 | reduce-window | flops 2080768 | bytes 131076 | tf_op jit(solution)/shard_map/reduce-window
  12.4 0.1 slice.14
  12.5 0.1 copy.13
  12.6 0.1 copy.14
  12.7 0.1 broadcast_add_fusion
  12.8 0.7 and_select_fusion.1
  13.5 0.6 add_select_fusion
  14.1 0.7 compare_select_fusion
  14.8 4.5 %scatter_custom_fusion.1 = s32[1280]{0:T(1024)S(1)} fusion(s32[1024]{0:T(1024)S(1)} %bitcast.79, s32[1024]{0:T(1024)} %bitcast.71, s32[]{:T(128)} %constant.43.clone.1), kind=kCustom, calls=%fused_computation.92 | custom fusion | bytes 5632 | tf_op jit(solution)/shard_map/scatter | solution.py:23
  19.4 0.1 broadcast_in_dim.69
  19.4 0.0 copy-done
  19.4 5.1 %gather_fusion.1 = bf16[1280,1024]{1,0:T(8,128)(2,1)} fusion(bf16[1024,1024]{1,0:T(8,128)(2,1)S(1)} %bitcast.63, s32[2048]{0:T(1024)S(1)} %pad_clamp_fusion), kind=kCustom, calls=%fused_computation.1 | custom fusion | bytes 5248000 | tf_op jit(solution)/shard_map/jit(_take)/gather | solution.py:25
  24.6 0.0 copy-start.2
  24.6 0.0 copy-start.5
  24.6 3.5 %broadcast_select_fusion = bf16[16,80,1024]{2,1,0:T(8,128)(2,1)} fusion(bf16[16,80,1024]{2,1,0:T(8,128)(2,1)} %bitcast.66, pred[16,80]{1,0:T(8,128)(4,1)S(1)} %broadcast_in_dim.69), kind=kLoop, calls=%fused_computation.60 | loop fusion | flops 1310720 | bytes 5244160 | tf_op jit(solution)/shard_map/jit(_take)/select_n | solution.py:25
  28.1 6.5 %all-to-all-start = ((bf16[16,80,1024]{2,1,0:T(8,128)(2,1)}), bf16[16,80,1024]{2,1,0:T(8,128)(2,1)}, u32[]{:S(2)}, u32[]{:S(2)}) async-start(bf16[16,80,1024]{2,1,0:T(8,128)(2,1)} %broadcast_select_fusion), calls=%async_computation | async-start | bytes 5242880 | tf_op jit(solution)/shard_map/all_to_all | solution.py:50
  34.6 0.0 copy-done.2
  34.7 0.0 copy-done.5
  34.7 58.9 %all-to-all-done = bf16[16,80,1024]{2,1,0:T(8,128)(2,1)} async-done(((bf16[16,80,1024]{2,1,0:T(8,128)(2,1)}), bf16[16,80,1024]{2,1,0:T(8,128)(2,1)}, u32[]{:S(2)}, u32[]{:S(2)}) %all-to-all-start) | async-done | bytes 2621472 | tf_op jit(solution)/shard_map/all_to_all | solution.py:50
  93.6 0.0 copy-start.6
  93.6 57.6 %fusion.2.clone.6 = bf16[1280,4096]{1,0:T(8,128)(2,1)S(1)} fusion(bf16[1280,1024]{1,0:T(8,128)(2,1)} %bitcast.13, f32[4096]{0:T(1024)S(1)} %bitcast.74, bf16[1,1024,4096]{2,1,0:T(8,128)(2,1)} %param.16), kind=kOutput, calls=%fused_computation.8.clone.clone.clone.clone.clone.1 | convolution fusion | flops 11083448320 | bytes 21512192 | tf_op jit(solution)/shard_map/dot_general | solution.py:30
  151.1 0.0 copy-done.6
  151.1 0.0 copy-start.4
  151.1 12.4 %add_convert_fusion = bf16[1280,1024]{1,0:T(8,128)(2,1)} fusion(bf16[1,4096,1024]{2,1,0:T(8,128)(2,1)S(1)} %copy-done.6, f32[1024]{0:T(1024)S(1)} %bitcast.78, bf16[1280,4096]{1,0:T(8,128)(2,1)S(1)} %fusion.2.clone.6), kind=kOutput, calls=%fused_computation.58 | convolution fusion | flops 10740039680 | bytes 21499904 | tf_op jit(solution)/shard_map/dot_general | solution.py:32
  163.6 0.0 copy-start.1
  163.6 5.0 %all-to-all-start.1 = ((bf16[16,80,1024]{2,1,0:T(8,128)(2,1)}), bf16[16,80,1024]{2,1,0:T(8,128)(2,1)}, u32[]{:S(2)}, u32[]{:S(2)}) async-start(bf16[16,80,1024]{2,1,0:T(8,128)(2,1)} %bitcast.67), calls=%async_computation.1 | async-start | bytes 5242880 | tf_op jit(solution)/shard_map/all_to_all | solution.py:52
  168.5 4.5 %scatter_custom_fusion = s32[1024]{0:T(1024)S(1)} fusion(s32[1024]{0:T(1024)} %bitcast.76, s32[1024]{0:T(1024)} %get-tuple-element.5, s32[]{:T(128)} %constant.42.clone.1), kind=kCustom, calls=%fused_computation.100 | custom fusion | bytes 4608 | tf_op jit(solution)/shard_map/scatter | solution.py:24
  173.0 1.8 multiply_reduce_fusion
  174.8 0.0 copy-done.4
  174.8 0.1 fusion.55
  175.6 0.2 fusion.94
  175.9 0.0 copy-done.1
  176.0 51.5 %all-to-all-done.1 = bf16[16,80,1024]{2,1,0:T(8,128)(2,1)} async-done(((bf16[16,80,1024]{2,1,0:T(8,128)(2,1)}), bf16[16,80,1024]{2,1,0:T(8,128)(2,1)}, u32[]{:S(2)}, u32[]{:S(2)}) %all-to-all-start.1) | async-done | bytes 2621472 | tf_op jit(solution)/shard_map/all_to_all | solution.py:52
  227.5 8.1 %gather_fusion.2 = bf16[1024,1024]{1,0:T(8,128)(2,1)} fusion(bf16[1280,1024]{1,0:T(8,128)(2,1)} %bitcast.19, s32[1024]{0:T(1024)S(1)} %fusion.59), kind=kCustom, calls=%fused_computation.2 | custom fusion | bytes 4198400 | tf_op jit(solution)/shard_map/jit(_take)/gather | solution.py:37
  235.5 3.5 %multiply_convert_fusion = bf16[1,1024,1024]{2,1,0:T(8,128)(2,1)} fusion(bf16[1024,1024]{1,0:T(8,128)(2,1)} %gather_fusion.2, f32[1024]{0:T(1024)S(1)} %select_reduce_fusion, pred[1024]{0:T(1024)(128)(4,1)S(1)} %compare_and_fusion.1), kind=kLoop, calls=%fused_computation.59 | loop fusion | flops 4194304 | bytes 4199424 | tf_op jit(solution)/shard_map/convert_element_type | solution.py:38
  (16 shorter events, 0.2 us)
Async XLA Ops:
  0.0 19.4 %copy-start = (bf16[1,1024,1024]{2,1,0:T(8,128)(2,1)S(1)}, bf16[1,1024,1024]{2,1,0:T(8,128)(2,1)}, u32[]{:S(2)}) copy-start(bf16[1,1024,1024]{2,1,0:T(8,128)(2,1)} %param.10) | copy-start | bytes 6291460
  0.8 0.6 copy-start.3
  24.6 10.1 %copy-start.2 = (bf16[1,4096]{1,0:T(2,128)(2,1)S(1)}, bf16[1,4096]{1,0:T(2,128)(2,1)}, u32[]{:S(2)}) copy-start(bf16[1,4096]{1,0:T(2,128)(2,1)} %param.17) | copy-start | bytes 24580
  24.6 10.1 %copy-start.5 = (bf16[1,1024]{1,0:T(2,128)(2,1)S(1)}, bf16[1,1024]{1,0:T(2,128)(2,1)}, u32[]{:S(2)}) copy-start(bf16[1,1024]{1,0:T(2,128)(2,1)} %param.19) | copy-start | bytes 6148
  28.1 65.5 %all-to-all-start = ((bf16[16,80,1024]{2,1,0:T(8,128)(2,1)}), bf16[16,80,1024]{2,1,0:T(8,128)(2,1)}, u32[]{:S(2)}, u32[]{:S(2)}) async-start(bf16[16,80,1024]{2,1,0:T(8,128)(2,1)} %broadcast_select_fusion), calls=%async_computation | async-start | bytes 5242880 | tf_op jit(solution)/shard_map/all_to_all | solution.py:50
  93.6 57.6 %copy-start.6 = (bf16[1,4096,1024]{2,1,0:T(8,128)(2,1)S(1)}, bf16[1,4096,1024]{2,1,0:T(8,128)(2,1)}, u32[]{:S(2)}) copy-start(bf16[1,4096,1024]{2,1,0:T(8,128)(2,1)} %param.18) | copy-start | bytes 25165828
  151.1 23.7 %copy-start.4 = (bf16[16,256]{1,0:T(8,128)(2,1)S(1)}, bf16[16,256]{1,0:T(8,128)(2,1)}, u32[]{:S(2)}) copy-start(bf16[16,256]{1,0:T(8,128)(2,1)} %param.14) | copy-start | bytes 24580
  163.6 12.3 %copy-start.1 = (s32[1,1024]{1,0:T(1,128)S(1)}, s32[1,1024]{1,0:T(1,128)}, u32[]{:S(2)}) copy-start(s32[1,1024]{1,0:T(1,128)} %param.11) | copy-start | bytes 12292
  163.6 63.9 %all-to-all-start.1 = ((bf16[16,80,1024]{2,1,0:T(8,128)(2,1)}), bf16[16,80,1024]{2,1,0:T(8,128)(2,1)}, u32[]{:S(2)}, u32[]{:S(2)}) async-start(bf16[16,80,1024]{2,1,0:T(8,128)(2,1)} %bitcast.67), calls=%async_computation.1 | async-start | bytes 5242880 | tf_op jit(solution)/shard_map/all_to_all | solution.py:52
where the time goes:
time: 240 us; the launch traced here: 239 us
  waiting for transfers between devices  110 us (46%)
  matrix products  72 us (30%)
  local copies, waits for them, and re-layouts  28.8 us (12%)
  other arithmetic  15.5 us (6%)
  starting transfers between devices  11.5 us (5%)
    all_to_all x1, waiting for transfers between devices, device_step(): lax.all_to_all(send_rows.reshape(num_experts, capacity, model_width), EXP...  58.9 us
    dot_general x1, matrix products, expert_local(): jnp.dot(slot_rows, w_first, preferred_element_type=jnp.float32)  57.6 us
    all_to_all x1, waiting for transfers between devices, device_step(): lax.all_to_all(expert_rows.reshape(num_experts, capacity, model_width), E...  51.5 us
    dot_general x1, matrix products, expert_local(): jnp.dot(hidden, w_second, preferred_element_type=jnp.float32)  12.4 us
    gather x1, local copies, waits for them, and re-layouts, combine_local(): picked = jnp.take(back_rows, dest_slot, axis=0, mode='fill', fill_value=0)  8.08 us
    all_to_all x1, starting transfers between devices, device_step(): lax.all_to_all(send_rows.reshape(num_experts, capacity, model_width), EXP...  6.52 us
    gather x1, local copies, waits for them, and re-layouts, route_local(): ranked_ids = jnp.take(id_row, order_row)  5.72 us
    gather x1, local copies, waits for them, and re-layouts, route_local(): jnp.take(tok_rows, slot_source, axis=0, mode='fill', fill_value=0)  5.12 us
  transfers between devices with their start and end apart: 2, of which 2 were waited for; matrix products, arithmetic and copies ran while one was open for 3% of the time, Pallas kernels for 0%

commit v1 on v0

v1 whole, which is shorter than its diff:
```python
import functools

import jax
import jax.numpy as jnp
from jax import lax
from jax.experimental import pallas as pl
from jax.experimental.pallas import tpu as pltpu
from jax.sharding import PartitionSpec as P

EXPERT_AXES = ("ep_b", "ep_a")
MESH = pl.DeviceIdType.MESH
F32, BF16, I32 = jnp.float32, jnp.bfloat16, jnp.int32
NT = (((1,), (1,)), ((), ()))


def xor(v, j, bits):
    total = 0
    for k in range(bits):
        total = total + lax.rem(lax.div(v, 1 << k) + lax.div(j, 1 << k), 2) * (1 << k)
    return total


def kernel(dims, tau_ref, ids_ref, order_ref, wr_hbm, keys_ref, b1_ref, b2_ref, tok_hbm, w1_hbm, w2_hbm, out_hbm,
           tok, wr, w1, w2, perm, send, recv, ybuf, back, hbuf, key_b, gate_b, acc, out,
           load_sem, out_sem, d_send, d_recv, r_send, r_recv):
    nb, na, cap = dims
    num_experts = nb * na
    half = num_experts // 2
    tok_dev, width = tok.shape
    hidden = w1.shape[1]
    dp = lax.axis_index("dp")
    my_b, my_a = lax.axis_index("ep_b"), lax.axis_index("ep_a")
    pair = 2 * cap

    def place(j):
        j = jnp.int32(j)
        return xor(my_b, lax.div(j, na), 2), xor(my_a, lax.rem(j, na), 2)

    def expert_of(j):
        b, a = place(j)
        return b * na + a

    def rows_of(slot):
        return pl.ds(pl.multiple_of(slot * cap, 16), cap)

    def exchange(src, dst, send_sem, recv_sem, slot, j):
        b, a = place(j)
        return pltpu.make_async_remote_copy(
            src_ref=src.at[rows_of(slot)], dst_ref=dst.at[rows_of(slot)],
            send_sem=send_sem.at[slot], recv_sem=recv_sem.at[slot],
            device_id=(dp, b, a), device_id_type=MESH)

    loads = [pltpu.make_async_copy(s, d, load_sem.at[k]) for k, (s, d) in enumerate(
        [(tok_hbm.at[0], tok), (wr_hbm, wr), (w1_hbm.at[0], w1), (w2_hbm.at[0], w2)])]
    for c in loads:
        c.start()
    barrier = pltpu.get_barrier_semaphore()

    def greet(j, carry):
        b, a = place(j)
        pl.semaphore_signal(barrier, inc=1, device_id=(dp, b, a), device_id_type=MESH)
        return carry

    lax.fori_loop(1, num_experts, greet, 0)

    ids = ids_ref[...]
    order = order_ref[...]
    hot = (lax.broadcasted_iota(I32, (num_experts, tok_dev), 0) == ids)
    hot_b = jnp.where(hot, 1.0, 0.0).astype(BF16)
    blk = 256
    for t in range(0, tok_dev, blk):
        o = (lax.broadcasted_iota(I32, (blk, tok_dev), 0) + t) == order
        perm[t:t + blk, :] = jnp.where(o, 1.0, 0.0).astype(BF16)
    ranked = jnp.dot(hot_b, perm[...], preferred_element_type=F32)
    tri = jnp.where(lax.broadcasted_iota(I32, (blk, blk), 0) <= lax.broadcasted_iota(I32, (blk, blk), 1), 1.0, 0.0).astype(BF16)
    carry = jnp.zeros((num_experts, 1), F32)
    pos = []
    for t in range(0, tok_dev, blk):
        part = ranked[:, t:t + blk]
        cum = jnp.dot(part.astype(BF16), tri, preferred_element_type=F32) + carry
        carry = cum[:, blk - 1:blk]
        pos.append(jnp.sum(cum * part, axis=0, keepdims=True) - 1.0)
    ranked_pos = jnp.minimum(jnp.concatenate(pos, axis=1), float(cap))
    pos_b = jnp.broadcast_to(ranked_pos, (16, tok_dev)).astype(BF16)
    slot_pos = lax.dot_general(pos_b, perm[...], NT, preferred_element_type=F32)[0:1, :]
    key_row = ids * 128 + slot_pos.astype(I32)

    loads[0].wait()
    row = lax.broadcasted_iota(I32, (pair, tok_dev), 0)

    def permute(i):
        far, near = expert_of(half + i), expert_of(i)
        target = jnp.where(row < cap, far * 128 + row, near * 128 + row - cap)
        one_hot = jnp.where(key_row == target, 1.0, 0.0).astype(BF16)
        return jnp.dot(one_hot, tok[...], preferred_element_type=F32).astype(BF16)

    def pair_rows(i):
        return pl.ds(pl.multiple_of(i * pair, 16), pair)

    first = permute(0)
    send[0:cap, :] = first[0:cap]
    recv[cap:pair, :] = first[cap:]
    send[pair:2 * pair, :] = permute(1)
    pl.semaphore_wait(barrier, num_experts - 1)
    exchange(send, recv, d_send, d_recv, 0, half).start()

    def dispatch(i, c):
        send[pair_rows(i + 1), :] = permute(i + 1)
        exchange(send, recv, d_send, d_recv, 2 * i, half + i).start()
        exchange(send, recv, d_send, d_recv, 2 * i + 1, i).start()
        return c

    lax.fori_loop(1, half - 1, dispatch, 0)

    loads[1].wait()
    keys_f32 = keys_ref[...].astype(F32)
    key_unit = keys_f32 / jnp.sqrt(jnp.sum(keys_f32 * keys_f32, axis=1, keepdims=True))
    tau = tau_ref[0, 0]
    exchange(send, recv, d_send, d_recv, num_experts - 2, num_experts - 1).start()
    exchange(send, recv, d_send, d_recv, num_experts - 1, half - 1).start()
    key_f = key_row.astype(F32)
    for t in range(0, tok_dev, blk):
        r = jnp.dot(tok[t:t + blk, :], wr[...], preferred_element_type=F32)
        unit = r / jnp.sqrt(jnp.sum(r * r, axis=1, keepdims=True))
        logits = lax.dot_general(key_unit, unit, NT, precision=lax.Precision.HIGHEST, preferred_element_type=F32) / tau
        e = jnp.exp(logits - jnp.max(logits, axis=0, keepdims=True))
        prob = e / jnp.sum(e, axis=0, keepdims=True)
        gate = jnp.sum(jnp.where(hot[:, t:t + blk], prob, 0.0), axis=0, keepdims=True)
        for s in range(0, blk, 128):
            gate_b[t + s:t + s + 128, :] = jnp.broadcast_to(gate[:, s:s + 128], (128, 128)).T
            column = jnp.broadcast_to(key_f[:, t + s:t + s + 128], (128, 128)).T
            key_b[t + s:t + s + 128, 0:128] = column
            key_b[t + s:t + s + 128, 128:256] = column

    loads[2].wait()
    loads[3].wait()

    def expert(i):
        x = recv[pair_rows(i), :]

        def first_layer(n, c):
            cols = pl.ds(pl.multiple_of(n * 512, 512), 512)
            h = jnp.dot(x, w1[:, cols], preferred_element_type=F32) + b1_ref[:, cols].astype(F32)
            h = 0.5 * h * (1.0 + lax.erf(h * 0.7071067811865476))
            hbuf[:, cols] = h.astype(BF16)
            return c

        lax.fori_loop(0, hidden // 512, first_layer, 0)

        def second_layer(n, c):
            cols = pl.ds(pl.multiple_of(n * 256, 256), 256)
            y = jnp.dot(hbuf[...], w2[:, cols], preferred_element_type=F32) + b2_ref[:, cols].astype(F32)
            ybuf[pair_rows(i), cols] = y.astype(BF16)
            return c

        lax.fori_loop(0, width // 256, second_layer, 0)

    exchange(send, recv, d_send, d_recv, 0, half).wait_recv()
    expert(0)
    exchange(ybuf, back, r_send, r_recv, 0, half).start()
    back[cap:pair, :] = ybuf[cap:pair, :]

    def process(i, c):
        exchange(send, recv, d_send, d_recv, 2 * i, half + i).wait_recv()
        exchange(send, recv, d_send, d_recv, 2 * i + 1, i).wait_recv()
        expert(i)
        exchange(ybuf, back, r_send, r_recv, 2 * i, half + i).start()
        exchange(ybuf, back, r_send, r_recv, 2 * i + 1, i).start()
        return c

    lax.fori_loop(1, half, process, 0)

    def picked(i, t):
        lane = lax.broadcasted_iota(I32, (1, pair), 1)
        far, near = expert_of(half + i), expert_of(i)
        target = jnp.where(lane < cap, far * 128 + lane, near * 128 + lane - cap).astype(F32)
        one_hot = jnp.where(key_b[t:t + blk, 0:pair] == target, 1.0, 0.0).astype(BF16)
        return jnp.dot(one_hot, back[pair_rows(i), :], preferred_element_type=F32)

    exchange(ybuf, back, r_send, r_recv, 0, half).wait_recv()
    for t in range(0, tok_dev, blk):
        acc[t:t + blk, :] = picked(0, t)

    def combine(i, c):
        exchange(ybuf, back, r_send, r_recv, 2 * i, half + i).wait_recv()
        exchange(ybuf, back, r_send, r_recv, 2 * i + 1, i).wait_recv()
        for t in range(0, tok_dev, blk):
            acc[t:t + blk, :] += picked(i, t)
        return c

    lax.fori_loop(1, half - 1, combine, 0)
    exchange(ybuf, back, r_send, r_recv, num_experts - 2, num_experts - 1).wait_recv()
    exchange(ybuf, back, r_send, r_recv, num_experts - 1, half - 1).wait_recv()
    stores = []
    for k, t in enumerate(range(0, tok_dev, blk)):
        total = acc[t:t + blk, :] + picked(half - 1, t)
        gate = gate_b[t:t + blk, :]
        for w in range(0, width, 128):
            out[t:t + blk, w:w + 128] = (gate * total[:, w:w + 128]).astype(BF16)
        stores.append(pltpu.make_async_copy(out.at[pl.ds(t, blk)], out_hbm.at[0, pl.ds(t, blk)], out_sem.at[k]))
        stores[-1].start()

    def drain(i, c):
        exchange(send, recv, d_send, d_recv, 2 * i, half + i).wait_send()
        exchange(ybuf, back, r_send, r_recv, 2 * i, half + i).wait_send()
        return c

    def drain_near(i, c):
        exchange(send, recv, d_send, d_recv, 2 * i + 1, i).wait_send()
        exchange(ybuf, back, r_send, r_recv, 2 * i + 1, i).wait_send()
        return c

    lax.fori_loop(0, half, drain, 0)
    lax.fori_loop(1, half, drain_near, 0)
    for c in stores:
        c.wait()


def solution(mesh):
    nb, na = mesh.shape["ep_b"], mesh.shape["ep_a"]
    num_experts = nb * na
    tok_spec = P(("dp",) + EXPERT_AXES)
    expert_spec = P(EXPERT_AXES)

    def device_step(tokens, expert_ids, route_order, w_route, expert_keys, value_a11, w_in, b_in, w_out, b_out):
        tok_dev, width = tokens.shape[1], tokens.shape[2]
        hidden = w_in.shape[2]
        cap = (5 * tok_dev + 4 * num_experts - 1) // (4 * num_experts)
        slots = num_experts * cap
        vmem = pl.BlockSpec(memory_space=pltpu.VMEM)
        hbm = pl.BlockSpec(memory_space=pl.ANY)
        smem = pl.BlockSpec(memory_space=pltpu.SMEM)
        dma = pltpu.SemaphoreType.DMA
        return pl.pallas_call(
            functools.partial(kernel, (nb, na, cap)),
            out_shape=jax.ShapeDtypeStruct((1, tok_dev, width), BF16),
            in_specs=[smem, vmem, vmem, hbm, vmem, vmem, vmem, hbm, hbm, hbm],
            out_specs=hbm,
            scratch_shapes=[
                pltpu.VMEM((tok_dev, width), BF16),
                pltpu.VMEM(w_route.shape, BF16),
                pltpu.VMEM((width, hidden), BF16),
                pltpu.VMEM((hidden, width), BF16),
                pltpu.VMEM((tok_dev, tok_dev), BF16),
                pltpu.VMEM((slots, width), BF16),
                pltpu.VMEM((slots, width), BF16),
                pltpu.VMEM((slots, width), BF16),
                pltpu.VMEM((slots, width), BF16),
                pltpu.VMEM((2 * cap, hidden), BF16),
                pltpu.VMEM((tok_dev, 256), F32),
                pltpu.VMEM((tok_dev, 128), F32),
                pltpu.VMEM((tok_dev, width), F32),
                pltpu.VMEM((tok_dev, width), BF16),
                dma((4,)),
                dma((4,)),
                dma((num_experts,)),
                dma((num_experts,)),
                dma((num_experts,)),
                dma((num_experts,)),
            ],
            compiler_params=pltpu.CompilerParams(collective_id=0, has_side_effects=True, vmem_limit_bytes=62 * 2**20),
            name="moe_exchange",
        )(value_a11.reshape(1, 1), expert_ids, route_order, w_route, expert_keys, b_in, b_out, tokens, w_in, w_out)

    return jax.shard_map(
        device_step,
        mesh=mesh,
        in_specs=(tok_spec, tok_spec, tok_spec, P(), P(), P(), expert_spec, expert_spec, expert_spec, expert_spec),
        out_specs=tok_spec,
        check_vma=False,
    )
```

time: 240 us -> 127 us (0.53)
  Pallas kernels: 0 us -> 123 us
  waiting for transfers between devices: 110 us -> 0 us
  matrix products: 72 us -> 0 us
  local copies, waits for them, and re-layouts: 28.8 us -> 3.08 us
  other arithmetic: 15.5 us -> 0 us
  starting transfers between devices: 11.5 us -> 0 us
    pallas_call x0 -> x1, Pallas kernels: none -> 123 us  [device_step(): pl.pallas_call(functools.partial(kernel, (nb, na, cap)), out_shape=jax.Sh...]
    all_to_all x2 -> x0, waiting for transfers between devices: 110 us -> none  [the longest x1 58.9 us: device_step(): lax.all_to_all(send_rows.reshape(num_experts, capacity, model_width), EXP...]
    dot_general x4 -> x0, matrix products: 72 us -> none  [the longest x1 57.6 us: expert_local(): jnp.dot(slot_rows, w_first, preferred_element_type=jnp.float32)]
    gather x3 -> x0, local copies, waits for them, and re-layouts: 18.9 us -> none  [the longest x1 8.08 us: combine_local(): picked = jnp.take(back_rows, dest_slot, axis=0, mode='fill', fill_value=0)]
    all_to_all x2 -> x0, starting transfers between devices: 11.5 us -> none  [the longest x1 6.52 us: device_step(): lax.all_to_all(send_rows.reshape(num_experts, capacity, model_width), EXP...]
    scatter x2 -> x0, local copies, waits for them, and re-layouts: 8.93 us -> none  [the longest x1 4.48 us: route_local(): jnp.full((num_experts * capacity,), tok_dev, jnp.int32).at[ranked_slot]]
    select_n x7 -> x0, other arithmetic: 7.07 us -> none  [the longest x2 3.54 us: route_local(): jnp.take(tok_rows, slot_source, axis=0, mode='fill', fill_value=0)]
    another operation x3 -> x0, other arithmetic: 4.64 us -> none
  transfers between devices with their start and end apart: 2 -> 0, of which waited for: 2 -> 0; matrix products, arithmetic and copies ran while one was open for 3% -> 0% of each run, Pallas kernels for 0% -> 0%
where the time goes in v1:
time: 127 us; the launch traced here: 126 us
  Pallas kernels  123 us (97%)
  local copies, waits for them, and re-layouts  3.08 us (2%)
    pallas_call x1, Pallas kernels, device_step(): pl.pallas_call(functools.partial(kernel, (nb, na, cap)), out_shape=jax.Sh...  123 us
    unnamed x1, local copies, waits for them, and re-layouts  3.08 us

profile of v1, /device:TPU:15, one launch (start us, length us, event | category | flops | bytes accessed | tf_op | source)
XLA Modules:
  0.0 126.4 jit_solution(3755957889790301138)
XLA Ops:
  0.7 122.6 %moe_exchange.1 = bf16[1,1024,1024]{2,1,0:T(8,128)(2,1)} custom-call(f32[1,1]{1,0:T(1,128)} %bitcast.1.tau_ref, s32[1,1024]{1,0:T(1,128)} %ids_ref.1, s32[1,1024]{1,0:T(1,128)} %order_ref.1, bf16[1024,256]{1,0:T(8,128)(2,1)} %wr_hbm.1, bf16[16,256]{1,0:T(8,128)(2,1)} %keys_ref.1, bf16[1,4096]{1,0:T(2,128)(2,1)} %b1_ref.1, bf16[1,1024]{1,0:T(2,128)(2,1)} %b2_ref.1, ...), custom_call_target="tpu_custom_call" | custom-call | tf_op jit(solution)/shard_map/moe_exchange/pallas_call | solution.py:234
  123.3 3.1 %copy.13 = bf16[1,1024,1024]{2,1,0:T(8,128)(2,1)} copy(bf16[1,1024,1024]{2,1,0:T(8,128)(2,1)} %moe_exchange.1) | data formatting | bytes 4194304

commit v2 on v1

--- a/solution.py
+++ b/solution.py
@@ -20,9 +20,10 @@
     return total
 
 
-def kernel(dims, tau_ref, ids_ref, order_ref, wr_hbm, keys_ref, b1_ref, b2_ref, tok_hbm, w1_hbm, w2_hbm, out_hbm,
-           tok, wr, w1, w2, perm, send, recv, ybuf, back, hbuf, key_b, gate_b, acc, out,
-           load_sem, out_sem, d_send, d_recv, r_send, r_recv):
+def kernel(dims, tau_hbm, ids_hbm, order_hbm, wr_hbm, keys_hbm, b1_hbm, b2_hbm, tok_hbm, w1_hbm, w2_hbm, out,
+           tau_ref, ids_ref, order_ref, keys_ref, b1_ref, b2_ref,
+           tok, wr, w1, w2, perm, send, recv, ybuf, back, hbuf, key_b, gate_b, acc, last,
+           load_sem, d_send, d_recv, r_send, r_recv):
     nb, na, cap = dims
     num_experts = nb * na
     half = num_experts // 2
@@ -50,10 +51,6 @@
             send_sem=send_sem.at[slot], recv_sem=recv_sem.at[slot],
             device_id=(dp, b, a), device_id_type=MESH)
 
-    loads = [pltpu.make_async_copy(s, d, load_sem.at[k]) for k, (s, d) in enumerate(
-        [(tok_hbm.at[0], tok), (wr_hbm, wr), (w1_hbm.at[0], w1), (w2_hbm.at[0], w2)])]
-    for c in loads:
-        c.start()
     barrier = pltpu.get_barrier_semaphore()
 
     def greet(j, carry):
@@ -62,7 +59,15 @@
         return carry
 
     lax.fori_loop(1, num_experts, greet, 0)
-
+    loads = [pltpu.make_async_copy(s, d, load_sem.at[k]) for k, (s, d) in enumerate([
+        (ids_hbm, ids_ref), (order_hbm, order_ref), (tok_hbm.at[0], tok),
+        (wr_hbm, wr), (keys_hbm, keys_ref), (tau_hbm, tau_ref), (b1_hbm, b1_ref), (b2_hbm, b2_ref),
+        (w1_hbm.at[0], w1), (w2_hbm.at[0], w2)])]
+    for c in loads:
+        c.start()
+
+    loads[0].wait()
+    loads[1].wait()
     ids = ids_ref[...]
     order = order_ref[...]
     hot = (lax.broadcasted_iota(I32, (num_experts, tok_dev), 0) == ids)
@@ -85,7 +90,7 @@
     slot_pos = lax.dot_general(pos_b, perm[...], NT, preferred_element_type=F32)[0:1, :]
     key_row = ids * 128 + slot_pos.astype(I32)
 
-    loads[0].wait()
+    loads[2].wait()
     row = lax.broadcasted_iota(I32, (pair, tok_dev), 0)
 
     def permute(i):
@@ -112,10 +117,11 @@
 
     lax.fori_loop(1, half - 1, dispatch, 0)
 
-    loads[1].wait()
+    for c in loads[3:6]:
+        c.wait()
     keys_f32 = keys_ref[...].astype(F32)
     key_unit = keys_f32 / jnp.sqrt(jnp.sum(keys_f32 * keys_f32, axis=1, keepdims=True))
-    tau = tau_ref[0, 0]
+    tau = tau_ref[0]
     exchange(send, recv, d_send, d_recv, num_experts - 2, num_experts - 1).start()
     exchange(send, recv, d_send, d_recv, num_experts - 1, half - 1).start()
     key_f = key_row.astype(F32)
@@ -132,8 +138,8 @@
             key_b[t + s:t + s + 128, 0:128] = column
             key_b[t + s:t + s + 128, 128:256] = column
 
-    loads[2].wait()
-    loads[3].wait()
+    for c in loads[6:]:
+        c.wait()
 
     def expert(i):
         x = recv[pair_rows(i), :]
@@ -170,12 +176,14 @@
 
     lax.fori_loop(1, half, process, 0)
 
-    def picked(i, t):
+    def selector(i, t):
         lane = lax.broadcasted_iota(I32, (1, pair), 1)
         far, near = expert_of(half + i), expert_of(i)
         target = jnp.where(lane < cap, far * 128 + lane, near * 128 + lane - cap).astype(F32)
-        one_hot = jnp.where(key_b[t:t + blk, 0:pair] == target, 1.0, 0.0).astype(BF16)
-        return jnp.dot(one_hot, back[pair_rows(i), :], preferred_element_type=F32)
+        return jnp.where(key_b[t:t + blk, 0:pair] == target, 1.0, 0.0).astype(BF16)
+
+    def picked(i, t):
+        return jnp.dot(selector(i, t), back[pair_rows(i), :], preferred_element_type=F32)
 
     exchange(ybuf, back, r_send, r_recv, 0, half).wait_recv()
     for t in range(0, tok_dev, blk):
@@ -189,16 +197,15 @@
         return c
 
     lax.fori_loop(1, half - 1, combine, 0)
+    for t in range(0, tok_dev, blk):
+        last[t:t + blk, :] = selector(half - 1, t)
+    exchange(ybuf, back, r_send, r_recv, num_experts - 1, half - 1).wait_recv()
     exchange(ybuf, back, r_send, r_recv, num_experts - 2, num_experts - 1).wait_recv()
-    exchange(ybuf, back, r_send, r_recv, num_experts - 1, half - 1).wait_recv()
-    stores = []
-    for k, t in enumerate(range(0, tok_dev, blk)):
-        total = acc[t:t + blk, :] + picked(half - 1, t)
+    for t in range(0, tok_dev, blk):
+        total = acc[t:t + blk, :] + jnp.dot(last[t:t + blk, :], back[pair_rows(half - 1), :], preferred_element_type=F32)
         gate = gate_b[t:t + blk, :]
         for w in range(0, width, 128):
-            out[t:t + blk, w:w + 128] = (gate * total[:, w:w + 128]).astype(BF16)
-        stores.append(pltpu.make_async_copy(out.at[pl.ds(t, blk)], out_hbm.at[0, pl.ds(t, blk)], out_sem.at[k]))
-        stores[-1].start()
+            out[0, t:t + blk, w:w + 128] = (gate * total[:, w:w + 128]).astype(BF16)
 
     def drain(i, c):
         exchange(send, recv, d_send, d_recv, 2 * i, half + i).wait_send()
@@ -212,8 +219,6 @@
 
     lax.fori_loop(0, half, drain, 0)
     lax.fori_loop(1, half, drain_near, 0)
-    for c in stores:
-        c.wait()
 
 
 def solution(mesh):
@@ -229,14 +234,19 @@
         slots = num_experts * cap
         vmem = pl.BlockSpec(memory_space=pltpu.VMEM)
         hbm = pl.BlockSpec(memory_space=pl.ANY)
-        smem = pl.BlockSpec(memory_space=pltpu.SMEM)
         dma = pltpu.SemaphoreType.DMA
         return pl.pallas_call(
             functools.partial(kernel, (nb, na, cap)),
-            out_shape=jax.ShapeDtypeStruct((1, tok_dev, width), BF16),
-            in_specs=[smem, vmem, vmem, hbm, vmem, vmem, vmem, hbm, hbm, hbm],
-            out_specs=hbm,
+            out_shape=pltpu.VMEM((1, tok_dev, width), BF16),
+            in_specs=[hbm] * 10,
+            out_specs=vmem,
             scratch_shapes=[
+                pltpu.SMEM((1,), F32),
+                pltpu.VMEM((1, tok_dev), I32),
+                pltpu.VMEM((1, tok_dev), I32),
+                pltpu.VMEM(expert_keys.shape, BF16),
+                pltpu.VMEM((1, hidden), BF16),
+                pltpu.VMEM((1, width), BF16),
                 pltpu.VMEM((tok_dev, width), BF16),
                 pltpu.VMEM(w_route.shape, BF16),
                 pltpu.VMEM((width, hidden), BF16),
@@ -250,17 +260,16 @@
                 pltpu.VMEM((tok_dev, 256), F32),
                 pltpu.VMEM((tok_dev, 128), F32),
                 pltpu.VMEM((tok_dev, width), F32),
-                pltpu.VMEM((tok_dev, width), BF16),
-                dma((4,)),
-                dma((4,)),
+                pltpu.VMEM((tok_dev, 2 * cap), BF16),
+                dma((10,)),
                 dma((num_experts,)),
                 dma((num_experts,)),
                 dma((num_experts,)),
                 dma((num_experts,)),
             ],
-            compiler_params=pltpu.CompilerParams(collective_id=0, has_side_effects=True, vmem_limit_bytes=62 * 2**20),
+            compiler_params=pltpu.CompilerParams(collective_id=0, has_side_effects=True, vmem_limit_bytes=56 * 2**20),
             name="moe_exchange",
-        )(value_a11.reshape(1, 1), expert_ids, route_order, w_route, expert_keys, b_in, b_out, tokens, w_in, w_out)
+        )(value_a11.reshape(1), expert_ids, route_order, w_route, expert_keys, b_in, b_out, tokens, w_in, w_out)
 
     return jax.shard_map(
         device_step,

time: 127 us -> 124 us (0.976)
  local copies, waits for them, and re-layouts: 3.08 us -> 1.32 us
    unnamed x1, local copies, waits for them, and re-layouts: 3.08 us -> 1.32 us
where the time goes in v2:
time: 124 us
  Pallas kernels  122 us (98%)
  local copies, waits for them, and re-layouts  1.32 us (1%)
    pallas_call x1, Pallas kernels, device_step(): pl.pallas_call(functools.partial(kernel, (nb, na, cap)), out_shape=pltpu....  122 us

profile of v2, /device:TPU:15, one launch (start us, length us, event | category | flops | bytes accessed | tf_op | source)
XLA Modules:
  0.0 124.1 jit_solution(3522456581072207727)
XLA Ops:
  0.7 122.1 %moe_exchange.1 = bf16[1,1024,1024]{2,1,0:T(8,128)(2,1)S(1)} custom-call(f32[1]{0:T(128)} %bitcast.1.tau_hbm, s32[1,1024]{1,0:T(1,128)} %ids_hbm.1, s32[1,1024]{1,0:T(1,128)} %order_hbm.1, bf16[1024,256]{1,0:T(8,128)(2,1)} %wr_hbm.1, bf16[16,256]{1,0:T(8,128)(2,1)} %keys_hbm.1, bf16[1,4096]{1,0:T(2,128)(2,1)} %b1_hbm.1, bf16[1,1024]{1,0:T(2,128)(2,1)} %b2_hbm.1, ...), custom_call_target="tpu_custom_call" | custom-call | tf_op jit(solution)/shard_map/moe_exchange/pallas_call | solution.py:238
  122.7 1.3 %copy.12 = bf16[1,1024,1024]{2,1,0:T(8,128)(2,1)} copy(bf16[1,1024,1024]{2,1,0:T(8,128)(2,1)S(1)} %moe_exchange.1) | data formatting | bytes 4194304

commit v3 on v2

v3 whole, which is shorter than its diff:
```python
import functools

import jax
import jax.numpy as jnp
from jax import lax
from jax.experimental import pallas as pl
from jax.experimental.pallas import tpu as pltpu
from jax.sharding import PartitionSpec as P

EXPERT_AXES = ("ep_b", "ep_a")
MESH = pl.DeviceIdType.MESH
F32, BF16, I32 = jnp.float32, jnp.bfloat16, jnp.int32
NT = (((1,), (1,)), ((), ()))
BLK, LANES = 256, 128


def one(mask, dtype=BF16):
    return jnp.where(mask, 1.0, 0.0).astype(dtype)


def xor(v, j, bits):
    total = 0
    for k in range(bits):
        total = total + lax.rem(lax.div(v, 1 << k) + lax.div(j, 1 << k), 2) * (1 << k)
    return total


def rank_tokens(ids, order, perm, num_experts, cap):
    tok_dev, blk = ids.shape[1], BLK
    hot = lax.broadcasted_iota(I32, (num_experts, tok_dev), 0) == ids
    hot_f = one(hot, F32)
    for t in range(0, tok_dev, blk):
        perm[t:t + blk, :] = one((lax.broadcasted_iota(I32, (blk, tok_dev), 0) + t) == order)
    ranked = jnp.dot(hot_f.astype(BF16), perm[...], preferred_element_type=F32)
    tri = one(lax.broadcasted_iota(I32, (blk, blk), 0) <= lax.broadcasted_iota(I32, (blk, blk), 1))
    count = jnp.zeros((num_experts, 1), F32)
    pos = []
    for t in range(0, tok_dev, blk):
        part = ranked[:, t:t + blk]
        cum = jnp.dot(part.astype(BF16), tri, preferred_element_type=F32) + count
        count = cum[:, blk - 1:]
        pos.append(jnp.sum(cum * part, axis=0, keepdims=True) - 1.0)
    ranked_pos = jnp.minimum(jnp.concatenate(pos, axis=1), float(cap))
    pos_b = jnp.broadcast_to(ranked_pos, (16, tok_dev)).astype(BF16)
    slot = lax.dot_general(pos_b, perm[...], NT, preferred_element_type=F32)[:1, :].astype(I32)
    return hot, hot_f, slot, count


def make_gates(tok, wr, keys_ref, tau, hot, gate_b, columns):
    keys_f32 = keys_ref[...].astype(F32)
    key_unit = keys_f32 / jnp.sqrt(jnp.sum(keys_f32 * keys_f32, axis=1, keepdims=True))
    for t in range(0, tok.shape[0], BLK):
        r = jnp.dot(tok[t:t + BLK, :], wr[...], preferred_element_type=F32)
        unit = r / jnp.sqrt(jnp.sum(r * r, axis=1, keepdims=True))
        logits = lax.dot_general(key_unit, unit, NT, precision=lax.Precision.HIGHEST, preferred_element_type=F32) / tau
        e = jnp.exp(logits - jnp.max(logits, axis=0, keepdims=True))
        prob = e / jnp.sum(e, axis=0, keepdims=True)
        gate = jnp.sum(jnp.where(hot[:, t:t + BLK], prob, 0.0), axis=0, keepdims=True)
        for s in range(0, BLK, LANES):
            rows = slice(t + s, t + s + LANES)
            gate_b[rows, :] = jnp.broadcast_to(gate[:, s:s + LANES], (LANES, LANES)).T
            for ref, row in columns:
                column = jnp.broadcast_to(row[:, rows], (LANES, LANES)).T
                ref[rows, :LANES] = column
                ref[rows, LANES:] = column


def run_expert(weights, src, dst, rows, size):
    w1, w2, b1_ref, b2_ref, hbuf = weights
    x = src[rows, :]

    def first_layer(n, c):
        cols = pl.ds(pl.multiple_of(n * 512, 512), 512)
        h = jnp.dot(x, w1[:, cols], preferred_element_type=F32) + b1_ref[:, cols].astype(F32)
        h = 0.5 * h * (1.0 + lax.erf(h * 0.7071067811865476))
        hbuf[:size, cols] = h.astype(BF16)
        return c

    lax.fori_loop(0, w1.shape[1] // 512, first_layer, 0)

    def second_layer(n, c):
        cols = pl.ds(pl.multiple_of(n * BLK, BLK), BLK)
        y = jnp.dot(hbuf[:size, :], w2[:, cols], preferred_element_type=F32) + b2_ref[:, cols].astype(F32)
        dst[rows, cols] = y.astype(BF16)
        return c

    lax.fori_loop(0, w2.shape[1] // BLK, second_layer, 0)


def full_kernel(dims, tau_hbm, ids_hbm, order_hbm, wr_hbm, keys_hbm, b1_hbm, b2_hbm, tok_hbm, w1_hbm, w2_hbm, out,
           tau_ref, ids_ref, order_ref, keys_ref, b1_ref, b2_ref,
           tok, wr, w1, w2, perm, send, recv, ybuf, back, hbuf, key_b, gate_b, acc, last,
           load_sem, d_send, d_recv, r_send, r_recv):
    nb, na, cap = dims
    num_experts = nb * na
    half = num_experts // 2
    tok_dev, width = tok.shape
    hidden = w1.shape[1]
    dp = lax.axis_index("dp")
    my_b, my_a = lax.axis_index("ep_b"), lax.axis_index("ep_a")
    pair = 2 * cap

    def place(j):
        j = jnp.int32(j)
        return xor(my_b, lax.div(j, na), 2), xor(my_a, lax.rem(j, na), 2)

    def expert_of(j):
        b, a = place(j)
        return b * na + a

    def rows_of(slot):
        return pl.ds(pl.multiple_of(slot * cap, 16), cap)

    def exchange(src, dst, send_sem, recv_sem, slot, j):
        b, a = place(j)
        return pltpu.make_async_remote_copy(
            src_ref=src.at[rows_of(slot)], dst_ref=dst.at[rows_of(slot)],
            send_sem=send_sem.at[slot], recv_sem=recv_sem.at[slot],
            device_id=(dp, b, a), device_id_type=MESH)

    barrier = pltpu.get_barrier_semaphore()

    def greet(j, carry):
        b, a = place(j)
        pl.semaphore_signal(barrier, inc=1, device_id=(dp, b, a), device_id_type=MESH)
        return carry

    lax.fori_loop(1, num_experts, greet, 0)
    loads = [pltpu.make_async_copy(s, d, load_sem.at[k]) for k, (s, d) in enumerate([
        (ids_hbm, ids_ref), (order_hbm, order_ref), (tok_hbm.at[0], tok),
        (wr_hbm, wr), (keys_hbm, keys_ref), (tau_hbm, tau_ref), (b1_hbm, b1_ref), (b2_hbm, b2_ref),
        (w1_hbm.at[0], w1), (w2_hbm.at[0], w2)])]
    for c in loads:
        c.start()

    loads[0].wait()
    loads[1].wait()
    blk = BLK
    hot, _, slot, _ = rank_tokens(ids_ref[...], order_ref[...], perm, num_experts, cap)
    key_row = ids_ref[...] * LANES + slot

    loads[2].wait()
    row = lax.broadcasted_iota(I32, (pair, tok_dev), 0)

    def permute(i):
        far, near = expert_of(half + i), expert_of(i)
        target = jnp.where(row < cap, far * LANES + row, near * LANES + row - cap)
        one_hot = one(key_row == target)
        return jnp.dot(one_hot, tok[...], preferred_element_type=F32).astype(BF16)

    def pair_rows(i):
        return pl.ds(pl.multiple_of(i * pair, 16), pair)

    first = permute(0)
    send[:cap, :] = first[:cap]
    recv[cap:pair, :] = first[cap:]
    send[pair:2 * pair, :] = permute(1)
    pl.semaphore_wait(barrier, num_experts - 1)
    exchange(send, recv, d_send, d_recv, 0, half).start()

    def dispatch(i, c):
        send[pair_rows(i + 1), :] = permute(i + 1)
        exchange(send, recv, d_send, d_recv, 2 * i, half + i).start()
        exchange(send, recv, d_send, d_recv, 2 * i + 1, i).start()
        return c

    lax.fori_loop(1, half - 1, dispatch, 0)

    for c in loads[3:6]:
        c.wait()
    exchange(send, recv, d_send, d_recv, num_experts - 2, num_experts - 1).start()
    exchange(send, recv, d_send, d_recv, num_experts - 1, half - 1).start()
    make_gates(tok, wr, keys_ref, tau_ref[0], hot, gate_b, [(key_b, key_row.astype(F32))])

    for c in loads[6:]:
        c.wait()

    def expert(i):
        run_expert((w1, w2, b1_ref, b2_ref, hbuf), recv, ybuf, pair_rows(i), pair)

    exchange(send, recv, d_send, d_recv, 0, half).wait_recv()
    expert(0)
    exchange(ybuf, back, r_send, r_recv, 0, half).start()
    back[cap:pair, :] = ybuf[cap:pair, :]

    def process(i, c):
        exchange(send, recv, d_send, d_recv, 2 * i, half + i).wait_recv()
        exchange(send, recv, d_send, d_recv, 2 * i + 1, i).wait_recv()
        expert(i)
        exchange(ybuf, back, r_send, r_recv, 2 * i, half + i).start()
        exchange(ybuf, back, r_send, r_recv, 2 * i + 1, i).start()
        return c

    lax.fori_loop(1, half, process, 0)

    def selector(i, t):
        lane = lax.broadcasted_iota(I32, (1, pair), 1)
        far, near = expert_of(half + i), expert_of(i)
        target = jnp.where(lane < cap, far * LANES + lane, near * LANES + lane - cap).astype(F32)
        return one(key_b[t:t + blk, :pair] == target)

    def picked(i, t):
        return jnp.dot(selector(i, t), back[pair_rows(i), :], preferred_element_type=F32)

    exchange(ybuf, back, r_send, r_recv, 0, half).wait_recv()
    for t in range(0, tok_dev, blk):
        acc[t:t + blk, :] = picked(0, t)

    def combine(i, c):
        exchange(ybuf, back, r_send, r_recv, 2 * i, half + i).wait_recv()
        exchange(ybuf, back, r_send, r_recv, 2 * i + 1, i).wait_recv()
        for t in range(0, tok_dev, blk):
            acc[t:t + blk, :] += picked(i, t)
        return c

    lax.fori_loop(1, half - 1, combine, 0)
    for t in range(0, tok_dev, blk):
        last[t:t + blk, :] = selector(half - 1, t)
    exchange(ybuf, back, r_send, r_recv, num_experts - 1, half - 1).wait_recv()
    exchange(ybuf, back, r_send, r_recv, num_experts - 2, num_experts - 1).wait_recv()
    for t in range(0, tok_dev, blk):
        total = acc[t:t + blk, :] + jnp.dot(last[t:t + blk, :], back[pair_rows(half - 1), :], preferred_element_type=F32)
        gate = gate_b[t:t + blk, :]
        for w in range(0, width, LANES):
            out[0, t:t + blk, w:w + LANES] = (gate * total[:, w:w + LANES]).astype(BF16)

    def drain(i, c):
        exchange(send, recv, d_send, d_recv, 2 * i, half + i).wait_send()
        exchange(ybuf, back, r_send, r_recv, 2 * i, half + i).wait_send()
        return c

    def drain_near(i, c):
        exchange(send, recv, d_send, d_recv, 2 * i + 1, i).wait_send()
        exchange(ybuf, back, r_send, r_recv, 2 * i + 1, i).wait_send()
        return c

    lax.fori_loop(0, half, drain, 0)
    lax.fori_loop(1, half, drain_near, 0)


def tight_kernel(dims, tau_hbm, ids_hbm, order_hbm, wr_hbm, keys_hbm, b1_hbm, b2_hbm, tok_hbm, w1_hbm, w2_hbm, out, flag_out,
                 tau_ref, ids_ref, order_ref, keys_ref, b1_ref, b2_ref,
                 tok, wr, w1, w2, perm, s_far, s_near, r_far, r_near, y_far, y_near, b_far, b_near,
                 p_send, p_recv, p_pack, p_back, o_send, o_recv, o_res, o_ret, meta_s, meta_r, flag_s, flag_r,
                 hbuf, key_b, q_b, gate_b, acc, unpack_ref,
                 load_sem, m_sem, p_sem, pb_sem, f_sem, df_send, df_recv, dn_send, dn_recv, do_send, do_recv,
                 rf_send, rf_recv, rn_send, rn_recv, ro_send, ro_recv):
    nb, na, cap, direct, packet = dims
    num_experts = nb * na
    half = num_experts // 2
    over = cap - direct
    steps = half // 2
    tok_dev, width = tok.shape
    hidden = w1.shape[1]
    dp = lax.axis_index("dp")
    my_b, my_a = lax.axis_index("ep_b"), lax.axis_index("ep_a")
    my_half = lax.div(my_b, nb // 2)
    blk = BLK

    def place(j):
        j = jnp.int32(j)
        return xor(my_b, lax.div(j, na), 2), xor(my_a, lax.rem(j, na), 2)

    def expert_of(j):
        b, a = place(j)
        return b * na + a

    def span(start, size):
        return pl.ds(pl.multiple_of(start, 16), size)

    def remote(src, dst, send_sem, recv_sem, j):
        b, a = place(j)
        return pltpu.make_async_remote_copy(src_ref=src, dst_ref=dst, send_sem=send_sem, recv_sem=recv_sem,
                                            device_id=(dp, b, a), device_id_type=MESH)

    def block(src, dst, send_sem, recv_sem, size, i, j):
        rows = span(i * size, size)
        return remote(src.at[rows], dst.at[rows], send_sem.at[i], recv_sem.at[i], j)

    def far_out(i):
        return block(s_far, r_far, df_send, df_recv, direct, i, half + i)

    def near_out(i):
        return block(s_near, r_near, dn_send, dn_recv, cap, i, i)

    def over_out(i):
        return block(o_send, o_recv, do_send, do_recv, over, i, i)

    def far_back(i):
        return block(y_far, b_far, rf_send, rf_recv, direct, i, half + i)

    def near_back(i):
        return block(y_near, b_near, rn_send, rn_recv, cap, i, i)

    def over_back(i):
        return block(o_res, o_ret, ro_send, ro_recv, over, i, i)

    meta_out = remote(meta_s, meta_r, m_sem.at[0], m_sem.at[1], half)
    packet_out = remote(p_send, p_recv, p_sem.at[0], p_sem.at[1], half)
    packet_back = remote(p_pack, p_back, pb_sem.at[0], pb_sem.at[1], half)
    rounds = [remote(flag_s.at[k], flag_r.at[k], f_sem.at[k, 0], f_sem.at[k, 1], j) for k, j in enumerate((4, 2, 1))]
    rounds.append(pltpu.make_async_remote_copy(
        src_ref=flag_s.at[3], dst_ref=flag_r.at[3], send_sem=f_sem.at[3, 0], recv_sem=f_sem.at[3, 1],
        device_id=(1 - dp, my_b, my_a), device_id_type=MESH))

    barrier = pltpu.get_barrier_semaphore()

    def greet(j, carry):
        b, a = place(j)
        pl.semaphore_signal(barrier, inc=1, device_id=(dp, b, a), device_id_type=MESH)
        return carry

    lax.fori_loop(1, num_experts, greet, 0)
    pl.semaphore_signal(barrier, inc=1, device_id=(1 - dp, my_b, my_a), device_id_type=MESH)
    loads = [pltpu.make_async_copy(s, d, load_sem.at[k]) for k, (s, d) in enumerate([
        (ids_hbm, ids_ref), (order_hbm, order_ref), (tok_hbm.at[0], tok),
        (wr_hbm, wr), (keys_hbm, keys_ref), (tau_hbm, tau_ref), (b1_hbm, b1_ref), (b2_hbm, b2_ref),
        (w1_hbm.at[0], w1), (w2_hbm.at[0], w2)])]
    for c in loads:
        c.start()

    loads[0].wait()
    loads[1].wait()
    ids = ids_ref[...]
    hot, hot_f, slot, count = rank_tokens(ids, order_ref[...], perm, num_experts, cap)
    key_row = ids * LANES + slot

    e_col = lax.broadcasted_iota(I32, (num_experts, 1), 0)
    extra = jnp.where(lax.div(e_col, half) != my_half, jnp.clip(count - float(direct), 0.0, float(over)), 0.0)
    extra_b = jnp.broadcast_to(extra, (num_experts, BLK))
    below = jnp.where(lax.broadcasted_iota(I32, (num_experts, num_experts), 1) < lax.broadcasted_iota(I32, (num_experts, num_experts), 0), 1.0, 0.0)
    base_b = jnp.dot(below.astype(BF16), extra_b.astype(BF16), preferred_element_type=F32)
    total_b = base_b[num_experts - 1:, :] + extra_b[num_experts - 1:, :]
    my_flag = jnp.broadcast_to(jnp.where(total_b > float(packet), 1.0, 0.0), (8, BLK))
    meta_s[:num_experts, :] = base_b
    meta_s[num_experts:2 * num_experts, :] = extra_b
    meta_s[2 * num_experts:, :] = my_flag
    base_tok = jnp.sum(hot_f * base_b[:, 0:1], axis=0, keepdims=True).astype(I32)
    is_extra = (lax.div(ids, half) != my_half) & (slot >= direct) & (slot < cap)
    q_row = jnp.where(is_extra, base_tok + slot - direct, -1)

    loads[2].wait()

    def gathered(mask):
        return jnp.dot(one(mask), tok[...], preferred_element_type=F32).astype(BF16)

    def two(first, second, size, axis, other):
        shape = (2 * size, other) if axis == 0 else (other, 2 * size)
        at = lax.broadcasted_iota(I32, shape, axis)
        return jnp.where(at < size, first * LANES + at, second * LANES + at - size)

    def far_keys(b, axis, other):
        return two(expert_of(half + 2 * b), expert_of(half + 2 * b + 1), direct, axis, other)

    def near_keys(b, axis, other):
        return two(expert_of(2 * b), expert_of(2 * b + 1), cap, axis, other)

    p_send[...] = gathered(lax.broadcasted_iota(I32, (packet, tok_dev), 0) == q_row)
    s_far[:2 * direct, :] = gathered(key_row == far_keys(0, 0, tok_dev))
    pl.semaphore_wait(barrier, num_experts)
    meta_out.start()
    packet_out.start()
    first = gathered(key_row == near_keys(0, 0, tok_dev))
    far_out(0).start()
    far_out(1).start()
    r_near[:cap, :] = first[:cap]
    s_near[cap:2 * cap, :] = first[cap:]

    def fill(b, c):
        s_far[span(2 * direct * b, 2 * direct), :] = gathered(key_row == far_keys(b, 0, tok_dev))
        s_near[span(2 * cap * b, 2 * cap), :] = gathered(key_row == near_keys(b, 0, tok_dev))
        return c

    lax.fori_loop(1, steps, fill, 0)

    for c in loads[3:6]:
        c.wait()
    make_gates(tok, wr, keys_ref, tau_ref[0], hot, gate_b, [(key_b, key_row.astype(F32)), (q_b, q_row.astype(F32))])

    meta_out.wait_recv()
    packet_out.wait_recv()
    q_lane = lax.broadcasted_iota(I32, (over, packet), 1).astype(F32)
    r_sub = lax.broadcasted_iota(I32, (over, packet), 0).astype(F32)
    picks = []
    lane = lax.broadcasted_iota(I32, (1, half * over), 1)
    home = jnp.full((1, half * over), -1.0, F32)
    for j in range(half):
        e = expert_of(j)
        base = meta_r[pl.ds(e, 1), :]
        size = meta_r[pl.ds(num_experts + e, 1), :]
        picks.append(one((q_lane - r_sub) == base[:, :packet]))
        at = (lane - j * over).astype(F32)
        home = jnp.where((at >= 0.0) & (at < size), base + at, home)
    forward = jnp.dot(jnp.concatenate(picks, axis=0), p_recv[...], preferred_element_type=F32).astype(BF16)
    o_recv[:over, :] = forward[:over]
    o_send[over:, :] = forward[over:]
    known = jnp.maximum(my_flag, meta_r[2 * num_experts:, :])
    flag_s[0] = known
    unpack = one(lax.broadcasted_iota(I32, (packet, half * over), 0).astype(F32) == home)

    def start_all(make):
        def go(i, c):
            make(i).start()
            return c
        lax.fori_loop(1, half, go, 0)

    start_all(over_out)
    rounds[0].start()
    near_out(1).start()

    def dispatch(b, c):
        for make, i in ((far_out, 2 * b), (near_out, 2 * b), (far_out, 2 * b + 1), (near_out, 2 * b + 1)):
            make(i).start()
        return c

    lax.fori_loop(1, steps, dispatch, 0)
    for c in loads[6:]:
        c.wait()

    def expert(src, dst, start, size):
        run_expert((w1, w2, b1_ref, b2_ref, hbuf), src, dst, span(start, size), size)

    def next_round(k):
        rounds[k].wait_recv()
        if k + 1 < len(rounds):
            flag_s[k + 1] = jnp.maximum(flag_s[k], flag_r[k])

    def step(b, c):
        far_out(2 * b).wait_recv()
        far_out(2 * b + 1).wait_recv()
        expert(r_far, y_far, 2 * direct * b, 2 * direct)
        far_back(2 * b).start()
        far_back(2 * b + 1).start()

        @pl.when(b > 0)
        def _():
            near_out(2 * b).wait_recv()

        near_out(2 * b + 1).wait_recv()
        expert(r_near, y_near, 2 * cap * b, 2 * cap)

        @pl.when(b > 0)
        def _():
            near_back(2 * b).start()

        near_back(2 * b + 1).start()

        @pl.when(b == 0)
        def _():
            def arrived(i, c):
                over_out(i).wait_recv()
                return c

            lax.fori_loop(1, half, arrived, 0)
            expert(o_recv, o_res, 0, half * over)
            o_ret[:over, :] = o_res[:over, :]
            start_all(over_back)

        @pl.when(b == 1)
        def _():
            next_round(0)
            rounds[1].start()

        return c

    unpack_ref[...] = unpack
    lax.fori_loop(0, steps, step, 0)
    b_near[:cap, :] = y_near[:cap, :]
    next_round(1)

    def returned(i, c):
        over_back(i).wait_recv()
        return c

    lax.fori_loop(1, half, returned, 0)
    p_pack[...] = jnp.dot(unpack_ref[...], o_ret[...], preferred_element_type=F32).astype(BF16)
    rounds[2].start()
    packet_back.start()

    def add(ref, start, keys, src, fresh=False):
        size = keys.shape[1]
        for t in range(0, tok_dev, blk):
            one_hot = one(ref[t:t + blk, :size] == keys)
            part = jnp.dot(one_hot, src[span(start, size), :], preferred_element_type=F32)
            acc[t:t + blk, :] = part if fresh else acc[t:t + blk, :] + part

    far_back(0).wait_recv()
    far_back(1).wait_recv()
    add(key_b, 0, far_keys(0, 1, 1).astype(F32), b_far, fresh=True)
    next_round(2)

    def near_sum(b, c):
        @pl.when(b > 0)
        def _():
            near_back(2 * b).wait_recv()
        near_back(2 * b + 1).wait_recv()
        add(key_b, 2 * cap * b, near_keys(b, 1, 1).astype(F32), b_near)
        return c

    lax.fori_loop(0, steps, near_sum, 0)
    rounds[3].start()

    def far_sum(b, c):
        far_back(2 * b).wait_recv()
        far_back(2 * b + 1).wait_recv()
        add(key_b, 2 * direct * b, far_keys(b, 1, 1).astype(F32), b_far)
        return c

    far_sum(1, 0)
    packet_back.wait_recv()
    add(q_b, 0, lax.broadcasted_iota(I32, (1, packet), 1).astype(F32), p_back)
    next_round(3)
    flag_s[4] = jnp.maximum(flag_s[3], flag_r[3])
    far_sum(2, 0)
    flag_out[0] = flag_s[4][0, 0].astype(I32)
    far_back(half - 2).wait_recv()
    far_back(half - 1).wait_recv()
    keys = far_keys(steps - 1, 1, 1).astype(F32)
    for t in range(0, tok_dev, blk):
        one_hot = one(key_b[t:t + blk, 0:2 * direct] == keys)
        total = acc[t:t + blk, :] + jnp.dot(one_hot, b_far[direct * (half - 2):, :], preferred_element_type=F32)
        gate = gate_b[t:t + blk, :]
        for w in range(0, width, LANES):
            out[0, t:t + blk, w:w + LANES] = (gate * total[:, w:w + LANES]).astype(BF16)

    def drain_far(i, c):
        far_out(i).wait_send()
        far_back(i).wait_send()
        return c

    def drain(i, c):
        near_out(i).wait_send()
        near_back(i).wait_send()
        over_out(i).wait_send()
        over_back(i).wait_send()
        return c

    lax.fori_loop(0, half, drain_far, 0)
    lax.fori_loop(1, half, drain, 0)
    for c in [meta_out, packet_out, packet_back] + rounds:
        c.wait_send()


def solution(mesh):
    nb, na = mesh.shape["ep_b"], mesh.shape["ep_a"]
    num_experts = nb * na
    half = num_experts // 2
    tok_spec = P(("dp",) + EXPERT_AXES)
    expert_spec = P(EXPERT_AXES)

    def device_step(tokens, expert_ids, route_order, w_route, expert_keys, value_a11, w_in, b_in, w_out, b_out):
        tok_dev, width = tokens.shape[1], tokens.shape[2]
        hidden = w_in.shape[2]
        cap = (5 * tok_dev + 4 * num_experts - 1) // (4 * num_experts)
        direct = 3 * tok_dev // (4 * num_experts)
        over = cap - direct
        packet = 11 * tok_dev // 64
        slots = num_experts * cap
        vmem = pl.BlockSpec(memory_space=pltpu.VMEM)
        hbm = pl.BlockSpec(memory_space=pl.ANY)
        dma = pltpu.SemaphoreType.DMA

        def rows(n, dtype=BF16, lanes=width):
            return pltpu.VMEM((n, lanes), dtype)

        operands = [
            pltpu.SMEM((1,), F32),
            rows(1, I32, tok_dev),
            rows(1, I32, tok_dev),
            rows(num_experts, BF16, expert_keys.shape[1]),
            rows(1, BF16, hidden),
            rows(1),
            rows(tok_dev),
            rows(width, BF16, w_route.shape[1]),
            rows(width, BF16, hidden),
            rows(hidden),
            rows(tok_dev, BF16, tok_dev),
        ]
        args = (value_a11.reshape(1), expert_ids, route_order, w_route, expert_keys, b_in, b_out, tokens, w_in, w_out)
        result = pltpu.VMEM((1, tok_dev, width), BF16)

        def full(*args):
            return pl.pallas_call(
                functools.partial(full_kernel, (nb, na, cap)),
                out_shape=result,
                in_specs=[hbm] * 10,
                out_specs=vmem,
                scratch_shapes=operands + [
                    rows(slots), rows(slots), rows(slots), rows(slots),
                    rows(2 * cap, BF16, hidden),
                    rows(tok_dev, F32, 256),
                    rows(tok_dev, F32, 128),
                    rows(tok_dev, F32),
                    rows(tok_dev, BF16, 2 * cap),
                    dma((10,)),
                ] + [dma((num_experts,))] * 4,
                compiler_params=pltpu.CompilerParams(collective_id=1, has_side_effects=True, vmem_limit_bytes=56 * 2**20),
                name="full_exchange",
            )(*args)

        far, near, extra = half * direct, half * cap, half * over
        out, flag = pl.pallas_call(
            functools.partial(tight_kernel, (nb, na, cap, direct, packet)),
            out_shape=(result, pltpu.SMEM((1,), I32)),
            in_specs=[hbm] * 10,
            out_specs=(vmem, pl.BlockSpec(memory_space=pltpu.SMEM)),
            scratch_shapes=operands + [
                rows(far), rows(near), rows(far), rows(near), rows(far), rows(near), rows(far), rows(near),
                rows(packet), rows(packet), rows(packet), rows(packet),
                rows(extra), rows(extra), rows(extra), rows(extra),
                rows(40, F32, 256), rows(40, F32, 256),
                pltpu.VMEM((5, 8, 256), F32), pltpu.VMEM((4, 8, 256), F32),
                rows(max(extra, 2 * cap), BF16, hidden),
                rows(tok_dev, F32, 256),
                rows(tok_dev, F32, 256),
                rows(tok_dev, F32, 128),
                rows(tok_dev, F32),
                rows(packet, BF16, extra),
                dma((10,)), dma((2,)), dma((2,)), dma((2,)), dma((4, 2)),
            ] + [dma((half,))] * 12,
            compiler_params=pltpu.CompilerParams(collective_id=0, has_side_effects=True, vmem_limit_bytes=61 * 2**20),
            name="tight_exchange",
        )(*args)
        return lax.cond(flag[0] > 0, lambda out, *args: full(*args), lambda out, *args: out, out, *args)

    return jax.shard_map(
        device_step,
        mesh=mesh,
        in_specs=(tok_spec, tok_spec, tok_spec, P(), P(), P(), expert_spec, expert_spec, expert_spec, expert_spec),
        out_specs=tok_spec,
        check_vma=False,
    )
```

time: 124 us -> 115 us (0.927)
  the two profiles are of different devices: /device:TPU:15 before, /device:TPU:1 now
where the time goes in v3:
time: 115 us
  Pallas kernels  113 us (98%)
  local copies, waits for them, and re-layouts  1.35 us (1%)
    pallas_call x1, Pallas kernels, device_step(): pl.pallas_call(functools.partial(tight_kernel, (nb, na, cap, direct, pack...  113 us

profile of v3, /device:TPU:1, one launch (start us, length us, event | category | flops | bytes accessed | tf_op | source)
XLA Modules:
  0.0 115.0 jit_solution(9159972866655617785)
XLA Ops:
  0.7 0.0 copy-start
  0.7 0.0 copy-start.1
  0.7 0.0 copy-start.2
  0.7 0.0 copy-start.3
  0.7 0.0 copy-start.4
  0.7 0.0 copy-start.5
  0.7 112.7 %tight_exchange.1 = (bf16[1,1024,1024]{2,1,0:T(8,128)(2,1)S(1)}, s32[1]{0:T(128)S(4)}) custom-call(f32[1]{0:T(128)} %bitcast.2.tau_hbm, s32[1,1024]{1,0:T(1,128)} %ids_hbm.1, s32[1,1024]{1,0:T(1,128)} %order_hbm.1, bf16[1024,256]{1,0:T(8,128)(2,1)} %wr_hbm.1, bf16[16,256]{1,0:T(8,128)(2,1)} %keys_hbm.1, bf16[1,4096]{1,0:T(2,128)(2,1)} %b1_hbm.1, ...), custom_call_target="tpu_custom_call" | custom-call | tf_op jit(solution)/shard_map/tight_exchange/pallas_call | solution.py:602
  113.4 0.0 copy-done
  113.4 0.0 copy-done.1
  113.4 0.0 copy-done.2
  113.4 0.0 copy-done.3
  113.4 0.0 copy-done.4
  113.4 0.0 copy-done.5
  113.5 0.2 conditional.1
  113.6 1.3 %copy.16 = bf16[1,1024,1024]{2,1,0:T(8,128)(2,1)} copy(bf16[1,1024,1024]{2,1,0:T(8,128)(2,1)S(1)} %get-tuple-element.43) | data formatting | bytes 4194304
Async XLA Ops:
  0.7 112.7 %copy-start = (bf16[1024,256]{1,0:T(8,128)(2,1)S(1)}, bf16[1024,256]{1,0:T(8,128)(2,1)}, u32[]{:S(2)}) copy-start(bf16[1024,256]{1,0:T(8,128)(2,1)} %wr_hbm.1) | copy-start | bytes 1572868
  0.7 112.7 %copy-start.1 = (bf16[1,4096]{1,0:T(2,128)(2,1)S(1)}, bf16[1,4096]{1,0:T(2,128)(2,1)}, u32[]{:S(2)}) copy-start(bf16[1,4096]{1,0:T(2,128)(2,1)} %b1_hbm.1) | copy-start | bytes 24580
  0.7 112.7 %copy-start.2 = (bf16[16,256]{1,0:T(8,128)(2,1)S(1)}, bf16[16,256]{1,0:T(8,128)(2,1)}, u32[]{:S(2)}) copy-start(bf16[16,256]{1,0:T(8,128)(2,1)} %keys_hbm.1) | copy-start | bytes 24580
  0.7 112.7 %copy-start.3 = (s32[1,1024]{1,0:T(1,128)S(1)}, s32[1,1024]{1,0:T(1,128)}, u32[]{:S(2)}) copy-start(s32[1,1024]{1,0:T(1,128)} %ids_hbm.1) | copy-start | bytes 12292
  0.7 112.7 %copy-start.4 = (s32[1,1024]{1,0:T(1,128)S(1)}, s32[1,1024]{1,0:T(1,128)}, u32[]{:S(2)}) copy-start(s32[1,1024]{1,0:T(1,128)} %order_hbm.1) | copy-start | bytes 12292
  0.7 112.7 %copy-start.5 = (bf16[1,1024]{1,0:T(2,128)(2,1)S(1)}, bf16[1,1024]{1,0:T(2,128)(2,1)}, u32[]{:S(2)}) copy-start(bf16[1,1024]{1,0:T(2,128)(2,1)} %b2_hbm.1) | copy-start | bytes 6148

commit v4 on v3

--- a/solution.py
+++ b/solution.py
@@ -250,6 +250,7 @@
     half = num_experts // 2
     over = cap - direct
     steps = half // 2
+    early = 1
     tok_dev, width = tok.shape
     hidden = w1.shape[1]
     dp = lax.axis_index("dp")
@@ -310,13 +311,13 @@
         pl.semaphore_signal(barrier, inc=1, device_id=(dp, b, a), device_id_type=MESH)
         return carry
 
-    lax.fori_loop(1, num_experts, greet, 0)
+    lax.fori_loop(1, num_experts, lambda k, c: greet(num_experts - k, c), 0)
     pl.semaphore_signal(barrier, inc=1, device_id=(1 - dp, my_b, my_a), device_id_type=MESH)
     loads = [pltpu.make_async_copy(s, d, load_sem.at[k]) for k, (s, d) in enumerate([
         (ids_hbm, ids_ref), (order_hbm, order_ref), (tok_hbm.at[0], tok),
         (wr_hbm, wr), (keys_hbm, keys_ref), (tau_hbm, tau_ref), (b1_hbm, b1_ref), (b2_hbm, b2_ref),
         (w1_hbm.at[0], w1), (w2_hbm.at[0], w2)])]
-    for c in loads:
+    for c in loads[:8]:
         c.start()
 
     loads[0].wait()
@@ -327,19 +328,25 @@
 
     e_col = lax.broadcasted_iota(I32, (num_experts, 1), 0)
     extra = jnp.where(lax.div(e_col, half) != my_half, jnp.clip(count - float(direct), 0.0, float(over)), 0.0)
-    extra_b = jnp.broadcast_to(extra, (num_experts, BLK))
+    extra_b = jnp.broadcast_to(extra, (num_experts, LANES))
     below = jnp.where(lax.broadcasted_iota(I32, (num_experts, num_experts), 1) < lax.broadcasted_iota(I32, (num_experts, num_experts), 0), 1.0, 0.0)
     base_b = jnp.dot(below.astype(BF16), extra_b.astype(BF16), preferred_element_type=F32)
     total_b = base_b[num_experts - 1:, :] + extra_b[num_experts - 1:, :]
-    my_flag = jnp.broadcast_to(jnp.where(total_b > float(packet), 1.0, 0.0), (8, BLK))
-    meta_s[:num_experts, :] = base_b
-    meta_s[num_experts:2 * num_experts, :] = extra_b
-    meta_s[2 * num_experts:, :] = my_flag
+    my_flag = jnp.broadcast_to(jnp.where(total_b > float(packet), 1.0, 0.0), (8, LANES))
+    diagonal = lax.broadcasted_iota(I32, (num_experts, LANES), 0) == lax.broadcasted_iota(I32, (num_experts, LANES), 1)
+
+    def as_row(column):
+        return jnp.sum(jnp.where(diagonal, column, 0.0), axis=0, keepdims=True)
+
+    kind = lax.broadcasted_iota(I32, meta_s.shape, 0)
+    meta_s[...] = jnp.where(kind == 0, as_row(base_b), jnp.where(kind == 1, as_row(extra_b), my_flag))
     base_tok = jnp.sum(hot_f * base_b[:, 0:1], axis=0, keepdims=True).astype(I32)
     is_extra = (lax.div(ids, half) != my_half) & (slot >= direct) & (slot < cap)
     q_row = jnp.where(is_extra, base_tok + slot - direct, -1)
 
     loads[2].wait()
+    for c in loads[8:]:
+        c.start()
 
     def gathered(mask):
         return jnp.dot(one(mask), tok[...], preferred_element_type=F32).astype(BF16)
@@ -372,6 +379,8 @@
         return c
 
     lax.fori_loop(1, steps, fill, 0)
+    for i in range(2, 2 * early):
+        far_out(i).start()
 
     for c in loads[3:6]:
         c.wait()
@@ -381,20 +390,20 @@
     packet_out.wait_recv()
     q_lane = lax.broadcasted_iota(I32, (over, packet), 1).astype(F32)
     r_sub = lax.broadcasted_iota(I32, (over, packet), 0).astype(F32)
+    e_lane = lax.broadcasted_iota(I32, (1, LANES), 1)
     picks = []
     lane = lax.broadcasted_iota(I32, (1, half * over), 1)
     home = jnp.full((1, half * over), -1.0, F32)
     for j in range(half):
         e = expert_of(j)
-        base = meta_r[pl.ds(e, 1), :]
-        size = meta_r[pl.ds(num_experts + e, 1), :]
-        picks.append(one((q_lane - r_sub) == base[:, :packet]))
+        base, size = (jnp.sum(jnp.where(e_lane == e, meta_r[k:k + 1, :], 0.0), axis=1, keepdims=True) for k in range(2))
+        picks.append(one((q_lane - r_sub) == base))
         at = (lane - j * over).astype(F32)
         home = jnp.where((at >= 0.0) & (at < size), base + at, home)
     forward = jnp.dot(jnp.concatenate(picks, axis=0), p_recv[...], preferred_element_type=F32).astype(BF16)
     o_recv[:over, :] = forward[:over]
     o_send[over:, :] = forward[over:]
-    known = jnp.maximum(my_flag, meta_r[2 * num_experts:, :])
+    known = jnp.maximum(my_flag, meta_r[2:3, :])
     flag_s[0] = known
     unpack = one(lax.broadcasted_iota(I32, (packet, half * over), 0).astype(F32) == home)
 
@@ -409,8 +418,13 @@
     near_out(1).start()
 
     def dispatch(b, c):
-        for make, i in ((far_out, 2 * b), (near_out, 2 * b), (far_out, 2 * b + 1), (near_out, 2 * b + 1)):
-            make(i).start()
+        @pl.when(b >= early)
+        def _():
+            far_out(2 * b).start()
+            far_out(2 * b + 1).start()
+
+        near_out(2 * b).start()
+        near_out(2 * b + 1).start()
         return c
 
     lax.fori_loop(1, steps, dispatch, 0)
@@ -445,7 +459,7 @@
 
         near_back(2 * b + 1).start()
 
-        @pl.when(b == 0)
+        @pl.when(b == 2)
         def _():
             def arrived(i, c):
                 over_out(i).wait_recv()
@@ -554,7 +568,7 @@
         cap = (5 * tok_dev + 4 * num_experts - 1) // (4 * num_experts)
         direct = 3 * tok_dev // (4 * num_experts)
         over = cap - direct
-        packet = 11 * tok_dev // 64
+        packet = 21 * tok_dev // 128
         slots = num_experts * cap
         vmem = pl.BlockSpec(memory_space=pltpu.VMEM)
         hbm = pl.BlockSpec(memory_space=pl.ANY)
@@ -608,8 +622,8 @@
                 rows(far), rows(near), rows(far), rows(near), rows(far), rows(near), rows(far), rows(near),
                 rows(packet), rows(packet), rows(packet), rows(packet),
                 rows(extra), rows(extra), rows(extra), rows(extra),
-                rows(40, F32, 256), rows(40, F32, 256),
-                pltpu.VMEM((5, 8, 256), F32), pltpu.VMEM((4, 8, 256), F32),
+                rows(8, F32, 128), rows(8, F32, 128),
+                pltpu.VMEM((5, 8, 128), F32), pltpu.VMEM((4, 8, 128), F32),
                 rows(max(extra, 2 * cap), BF16, hidden),
                 rows(tok_dev, F32, 256),
                 rows(tok_dev, F32, 256),

time: 115 us -> 113 us (0.983)
  the two profiles are of different devices: /device:TPU:1 before, /device:TPU:0 now
where the time goes in v4:
time: 113 us; the launch traced here: 112 us
  Pallas kernels  110 us (97%)
  local copies, waits for them, and re-layouts  1.35 us (1%)
    pallas_call x1, Pallas kernels, device_step(): pl.pallas_call(functools.partial(tight_kernel, (nb, na, cap, direct, pack...  110 us

profile of v4, /device:TPU:0, one launch (start us, length us, event | category | flops | bytes accessed | tf_op | source)
XLA Modules:
  0.0 112.4 jit_solution(11633259641846937174)
XLA Ops:
  0.7 0.0 copy-start
  0.7 0.0 copy-start.1
  0.7 0.0 copy-start.2
  0.7 0.0 copy-start.3
  0.7 0.0 copy-start.4
  0.7 0.0 copy-start.5
  0.7 110.1 %tight_exchange.1 = (bf16[1,1024,1024]{2,1,0:T(8,128)(2,1)S(1)}, s32[1]{0:T(128)S(4)}) custom-call(f32[1]{0:T(128)} %bitcast.2.tau_hbm, s32[1,1024]{1,0:T(1,128)} %ids_hbm.1, s32[1,1024]{1,0:T(1,128)} %order_hbm.1, bf16[1024,256]{1,0:T(8,128)(2,1)} %wr_hbm.1, bf16[16,256]{1,0:T(8,128)(2,1)} %keys_hbm.1, bf16[1,4096]{1,0:T(2,128)(2,1)} %b1_hbm.1, ...), custom_call_target="tpu_custom_call" | custom-call | tf_op jit(solution)/shard_map/tight_exchange/pallas_call | solution.py:616
  110.8 0.0 copy-done
  110.8 0.0 copy-done.1
  110.8 0.0 copy-done.2
  110.8 0.0 copy-done.3
  110.9 0.0 copy-done.4
  110.9 0.0 copy-done.5
  110.9 0.2 conditional.1
  111.1 1.3 %copy.16 = bf16[1,1024,1024]{2,1,0:T(8,128)(2,1)} copy(bf16[1,1024,1024]{2,1,0:T(8,128)(2,1)S(1)} %get-tuple-element.43) | data formatting | bytes 4194304
Async XLA Ops:
  0.7 110.2 %copy-start = (bf16[1024,256]{1,0:T(8,128)(2,1)S(1)}, bf16[1024,256]{1,0:T(8,128)(2,1)}, u32[]{:S(2)}) copy-start(bf16[1024,256]{1,0:T(8,128)(2,1)} %wr_hbm.1) | copy-start | bytes 1572868
  0.7 110.2 %copy-start.1 = (bf16[1,4096]{1,0:T(2,128)(2,1)S(1)}, bf16[1,4096]{1,0:T(2,128)(2,1)}, u32[]{:S(2)}) copy-start(bf16[1,4096]{1,0:T(2,128)(2,1)} %b1_hbm.1) | copy-start | bytes 24580
  0.7 110.2 %copy-start.2 = (bf16[16,256]{1,0:T(8,128)(2,1)S(1)}, bf16[16,256]{1,0:T(8,128)(2,1)}, u32[]{:S(2)}) copy-start(bf16[16,256]{1,0:T(8,128)(2,1)} %keys_hbm.1) | copy-start | bytes 24580
  0.7 110.2 %copy-start.3 = (s32[1,1024]{1,0:T(1,128)S(1)}, s32[1,1024]{1,0:T(1,128)}, u32[]{:S(2)}) copy-start(s32[1,1024]{1,0:T(1,128)} %ids_hbm.1) | copy-start | bytes 12292
  0.7 110.2 %copy-start.4 = (s32[1,1024]{1,0:T(1,128)S(1)}, s32[1,1024]{1,0:T(1,128)}, u32[]{:S(2)}) copy-start(s32[1,1024]{1,0:T(1,128)} %order_hbm.1) | copy-start | bytes 12292
  0.7 110.2 %copy-start.5 = (bf16[1,1024]{1,0:T(2,128)(2,1)S(1)}, bf16[1,1024]{1,0:T(2,128)(2,1)}, u32[]{:S(2)}) copy-start(bf16[1,1024]{1,0:T(2,128)(2,1)} %b2_hbm.1) | copy-start | bytes 6148
